TPU v7x, 128 devices: a whole 4x4x4 slice. The times are simulated.
128 devices in a mesh: node: 32 (over x, z, core), feat: 4 (over y).
Axes of the slice: x: 4, y: 4, z: 4, core: 2. Of those that a mesh axis runs over, the one named last changes fastest.
Arguments:
- features: bfloat16 [100, 32768], P('feat', 'node'), may hold values from -6 to 6
- edges_one: int32 [1024, 32768], P(None, 'node'), may hold values from 0 to 1, as said below
- w1_self: bfloat16 [100, 256], P('feat'), may hold values from -0.625 to 0.625
- w1_nbr: bfloat16 [100, 256], P('feat'), may hold values from -1.25 to 1.25
- need_blocks: int32 [32, 4], P('node'), may hold values from 0 to 31, as said below
- live_slots: int32 [32, 4], P('node'), may hold values from 0 to 1, as said below
- edges_two: int32 [4096, 32768], P(None, 'node'), may hold values from 0 to 1, as said below
- w2_self: bfloat16 [256, 47], P('feat'), may hold values from -0.375 to 0.375
- w2_nbr: bfloat16 [256, 47], P('feat'), may hold values from -0.5 to 0.5
- labels: int32 [32768], P('node'), may hold values from 0 to 46
Outputs:
- node_loss: float32 [32768], P('node')
- mean_loss: float32 [], replicated
Inputs may be any that keep to these rules, and one draw needn't show every extreme that they name: `need_blocks`: row b holds 4 different blocks; its first entry is b, its second is b plus half the number of blocks, its third is b minus 1, and its entry k is b plus an offset that depends on k alone, modulo the number of blocks. `live_slots`: the first three entries of each row are 1. `edges_one`: each column has exactly 25 ones. `edges_two`: each column t has exactly 10 ones, all in rows of slots that live_slots marks as used for t's block.
All inputs are finite; a program needn't handle non-finite values.
Results may differ from a plain program's by a relative error of at most 0.00065.
Values may be sent and summed in bfloat16 or wider, within the bound.
A program may use at most 128 MiB of HBM per device.

v0:
```python
import jax
import jax.numpy as jnp
from jax import lax
from jax.sharding import PartitionSpec as P

FAN1 = 25
FAN2 = 10


def from_behind(value, axis, steps):
    count = lax.axis_size(axis)
    pairs = [(source, (source + steps) % count) for source in range(count)]
    return lax.ppermute(value, axis, pairs)


def split_up(value, dim, devices):
    dims = value.shape
    parts = value.reshape(*dims[:dim], devices, dims[dim] // devices, *dims[dim + 1 :])
    return jnp.moveaxis(parts, dim, 0)


def sum_at_owner(value, axis, dim):
    devices = lax.axis_size(axis)
    parts = lax.all_to_all(split_up(value, dim, devices), axis, 0, 0, tiled=True)
    return jnp.sum(parts, axis=0)


def from_everyone(value, axis):
    devices = lax.axis_size(axis)
    return lax.all_to_all(
        jnp.broadcast_to(value[None], (devices, *value.shape)), axis, 0, 0, tiled=True
    )


def taken_together(value, axis):
    everything = from_everyone(value, axis)
    return jnp.sum(everything, axis=0)


def contract(weight, values):
    return lax.dot_general(
        weight, values, (((0,), (0,)), ((), ())), preferred_element_type=jnp.float32
    )


def contract_exact(weight, values):
    return lax.dot_general(
        weight,
        values,
        (((0,), (0,)), ((), ())),
        precision=lax.Precision.HIGHEST,
        preferred_element_type=jnp.float32,
    )


def fetch_offset(hidden, offset):
    nodes = lax.axis_size("node")
    levels = nodes.bit_length() - 1
    carried = hidden
    for level_bit in range(levels):
        moved = from_behind(carried, "node", nodes - (1 << level_bit))
        carried = jnp.where(offset // (1 << level_bit) % 2 == 1, moved, carried)
    return carried


def local(
    features,
    edges_one,
    w1_self,
    w1_nbr,
    need_blocks,
    live_slots,
    edges_two,
    w2_self,
    w2_nbr,
    labels,
):
    block_len = features.shape[1]
    classes = w2_self.shape[1]
    adjacency = edges_one.astype(jnp.bfloat16)
    neighbour = (jnp.dot(features, adjacency, preferred_element_type=jnp.float32) / FAN1).astype(
        jnp.bfloat16
    )
    before = sum_at_owner(contract(w1_self, features) + contract(w1_nbr, neighbour), "feat", 0)
    hidden = jax.nn.relu(before).astype(jnp.bfloat16)
    need_row = need_blocks[0]
    live_row = live_slots[0]
    self_term = contract(w2_self, hidden)
    nodes = lax.axis_size("node")
    mine_index = lax.axis_index("node")
    first_rows = edges_two[0:block_len].astype(jnp.bfloat16)
    gathered = jnp.dot(hidden, first_rows, preferred_element_type=jnp.float32)
    for slot in range(1, need_row.shape[0]):
        offset = (need_row[slot] - mine_index + nodes) % nodes
        sources = fetch_offset(hidden, offset)
        rows = edges_two[slot * block_len : (slot + 1) * block_len].astype(jnp.bfloat16)
        term = jnp.dot(sources, rows, preferred_element_type=jnp.float32)
        gathered = gathered + jnp.where(live_row[slot] == 1, term, 0.0)
    neighbour_term = contract_exact(w2_nbr.astype(jnp.float32), gathered)
    logits = taken_together(self_term + neighbour_term / FAN2, "feat")
    class_ids = jnp.arange(classes, dtype=jnp.int32)[:, None]
    picked = jnp.sum(jnp.where(class_ids == labels[None, :], logits, 0.0), 0)
    node_loss = jnp.log(jnp.sum(jnp.exp(logits), 0)) - picked
    summed = taken_together(jnp.sum(node_loss), "node")
    mean_loss = summed / (block_len * lax.axis_size("node"))
    return (node_loss, mean_loss)


def solution(mesh):
    return jax.shard_map(
        local,
        mesh=mesh,
        in_specs=(
            P("feat", "node"),
            P(None, "node"),
            P("feat", None),
            P("feat", None),
            P("node", None),
            P("node", None),
            P(None, "node"),
            P("feat", None),
            P("feat", None),
            P("node"),
        ),
        out_specs=(P("node"), P()),
        check_vma=False,
    )
```

profile of v0, /device:TPU:1, one launch (start us, length us, event | category | flops | bytes accessed | tf_op | source)
XLA Modules:
  0.0 120.8 jit_solution(14918321920840952772)
XLA Ops:
  0.6 0.8 copy-done
  1.5 1.0 fusion.49
  2.5 2.9 %fusion.10 = f32[256,1024]{1,0:T(8,128)S(1)} fusion(f32[256,1024]{1,0:T(8,128)S(1)} %fusion.49, bf16[25,256]{1,0:T(8,128)(2,1)} %param.13, bf16[25,1024]{1,0:T(8,128)(2,1)S(1)} %copy-done, s32[1024,1024]{1,0:T(8,128)} %param.11), kind=kOutput, calls=%fused_computation.11 | convolution fusion | flops 66897920 | bytes 6355456 | tf_op jit(solution)/shard_map/dot_general | solution.py:41
  5.4 19.0 %all_to_all.16 = f32[4,64,1024]{2,1,0:T(8,128)S(1)} all-to-all(f32[4,64,1024]{2,1,0:T(8,128)S(1)} %bitcast.20), channel_id=1, replica_groups=mesh['node'=32,'feat'=4] {'feat'}, dimensions={0} | all-to-all | bytes 2097152 | tf_op jit(solution)/shard_map/all_to_all | solution.py:24
  24.5 1.9 %collective-permute-start = (bf16[64,1024]{1,0:T(8,128)(2,1)S(1)}, bf16[64,1024]{1,0:T(8,128)(2,1)S(1)}, u32[]{:S(2)}, u32[]{:S(2)}) collective-permute-start(bf16[64,1024]{1,0:T(8,128)(2,1)S(1)} %maximum_convert_fusion), channel_id=1, source_target_pairs={{0,124},{4,0},{8,4},{12,8},{16,12},{20,16},{24,20},{28,24},{32,28}... | collective-permute-start | bytes 393224 | tf_op jit(solution)/shard_map/ppermute | solution.py:13
  29.3 9.6 %convert.6 = bf16[4096,1024]{1,0:T(8,128)(2,1)} convert(s32[4096,1024]{1,0:T(8,128)} %param.16) | non-fusion elementwise | flops 4194304 | bytes 25165824 | tf_op jit(solution)/shard_map/convert.3
  39.0 0.6 fusion.47
  41.7 6.0 %collective-permute-start.1 = (bf16[64,1024]{1,0:T(8,128)(2,1)S(1)}, bf16[64,1024]{1,0:T(8,128)(2,1)S(1)}, u32[]{:S(2)}, u32[]{:S(2)}) collective-permute-start(bf16[64,1024]{1,0:T(8,128)(2,1)S(1)} %get-tuple-element.6), channel_id=1, source_target_pairs={{0,120},{4,124},{8,0},{12,4},{16,8},{20,12},{24,16},{28,20},{32,24... | collective-permute-start | bytes 393224 | tf_op jit(solution)/shard_map/ppermute | solution.py:13
  47.7 2.1 %fusion.6 = f32[64,1024]{1,0:T(8,128)S(1)} fusion(bf16[4096,1024]{1,0:T(8,128)(2,1)} %convert.6, bf16[64,1024]{1,0:T(8,128)(2,1)S(1)} %reduce_sum.54), kind=kOutput, calls=%fused_computation.6 | convolution fusion | flops 134414336 | bytes 2490368 | tf_op jit(solution)/shard_map/dot_general | solution.py:92
  50.6 2.9 %collective-permute-start.2 = (bf16[64,1024]{1,0:T(8,128)(2,1)S(1)}, bf16[64,1024]{1,0:T(8,128)(2,1)S(1)}, u32[]{:S(2)}, u32[]{:S(2)}) collective-permute-start(bf16[64,1024]{1,0:T(8,128)(2,1)S(1)} %broadcast_select_fusion.9), channel_id=1, source_target_pairs={{0,112},{4,116},{8,120},{12,124},{16,0},{20,4},{24,8},{28,12},{32,... | collective-permute-start | bytes 393224 | tf_op jit(solution)/shard_map/ppermute | solution.py:13
  54.0 1.4 %collective-permute-start.6 = (bf16[64,1024]{1,0:T(8,128)(2,1)S(1)}, bf16[64,1024]{1,0:T(8,128)(2,1)S(1)}, u32[]{:S(2)}, u32[]{:S(2)}) collective-permute-start(bf16[64,1024]{1,0:T(8,128)(2,1)S(1)} %broadcast_select_fusion.5), channel_id=1, source_target_pairs={{0,112},{4,116},{8,120},{12,124},{16,0},{20,4},{24,8},{28,12},{32,... | collective-permute-start | bytes 393224 | tf_op jit(solution)/shard_map/ppermute | solution.py:13
  55.5 8.4 %collective-permute-done.9 = bf16[64,1024]{1,0:T(8,128)(2,1)S(1)} collective-permute-done((bf16[64,1024]{1,0:T(8,128)(2,1)S(1)}, bf16[64,1024]{1,0:T(8,128)(2,1)S(1)}, u32[]{:S(2)}, u32[]{:S(2)}) %collective-permute-start.9) | collective-permute-done | bytes 131104 | tf_op jit(solution)/shard_map/ppermute | solution.py:13
  64.2 6.0 %collective-permute-done.10 = bf16[64,1024]{1,0:T(8,128)(2,1)S(1)} collective-permute-done((bf16[64,1024]{1,0:T(8,128)(2,1)S(1)}, bf16[64,1024]{1,0:T(8,128)(2,1)S(1)}, u32[]{:S(2)}, u32[]{:S(2)}) %collective-permute-start.10) | collective-permute-done | bytes 131104 | tf_op jit(solution)/shard_map/ppermute | solution.py:13
  70.4 2.0 %collective-permute-done.7 = bf16[64,1024]{1,0:T(8,128)(2,1)S(1)} collective-permute-done((bf16[64,1024]{1,0:T(8,128)(2,1)S(1)}, bf16[64,1024]{1,0:T(8,128)(2,1)S(1)}, u32[]{:S(2)}, u32[]{:S(2)}) %collective-permute-start.7) | collective-permute-done | bytes 131104 | tf_op jit(solution)/shard_map/ppermute | solution.py:13
  72.4 1.1 collective-permute-start.8
  73.5 2.8 %collective-permute-done.11 = bf16[64,1024]{1,0:T(8,128)(2,1)S(1)} collective-permute-done((bf16[64,1024]{1,0:T(8,128)(2,1)S(1)}, bf16[64,1024]{1,0:T(8,128)(2,1)S(1)}, u32[]{:S(2)}, u32[]{:S(2)}) %collective-permute-start.11) | collective-permute-done | bytes 131104 | tf_op jit(solution)/shard_map/ppermute | solution.py:13
  76.4 1.5 %collective-permute-done.8 = bf16[64,1024]{1,0:T(8,128)(2,1)S(1)} collective-permute-done((bf16[64,1024]{1,0:T(8,128)(2,1)S(1)}, bf16[64,1024]{1,0:T(8,128)(2,1)S(1)}, u32[]{:S(2)}, u32[]{:S(2)}) %collective-permute-start.8) | collective-permute-done | bytes 131104 | tf_op jit(solution)/shard_map/ppermute | solution.py:13
  77.8 2.1 %fusion.20 = f32[64,1024]{1,0:T(8,128)S(1)} fusion(bf16[4096,1024]{1,0:T(8,128)(2,1)} %convert.6, bf16[64,1024]{1,0:T(8,128)(2,1)S(1)} %collective-permute-done.8, bf16[64,1024]{1,0:T(8,128)(2,1)S(1)} %broadcast_select_fusion.7, pred[]{:T(512)S(6)} %eq.104, pred[]{:T(512)} %bitcast.4), kind=kOutput, calls=%fused_computation.15 | convolution fusion | flops 134348800 | bytes 2621953 | tf_op jit(solution)/shard_map/dot_general | solution.py:97
  79.9 1.7 %collective-permute-done.12 = bf16[64,1024]{1,0:T(8,128)(2,1)S(1)} collective-permute-done((bf16[64,1024]{1,0:T(8,128)(2,1)S(1)}, bf16[64,1024]{1,0:T(8,128)(2,1)S(1)}, u32[]{:S(2)}, u32[]{:S(2)}) %collective-permute-start.12) | collective-permute-done | bytes 131104 | tf_op jit(solution)/shard_map/ppermute | solution.py:13
  83.2 10.7 %all_to_all.17 = f32[4,47,1024]{2,1,0:T(8,128)S(1)} all-to-all(f32[4,47,1024]{2,1,0:T(8,128)S(1)} %broadcast_in_dim.12), channel_id=1, replica_groups=mesh['node'=32,'feat'=4] {'feat'}, dimensions={0} | all-to-all | bytes 1540096 | tf_op jit(solution)/shard_map/all_to_all | solution.py:30
  94.1 1.2 fusion.46
  95.3 0.7 broadcast_in_dim.24
  96.0 22.4 %all_to_all.18 = f32[32,1,1]{2,1,0:T(1,128)S(1)} all-to-all(f32[32,1,1]{2,1,0:T(1,128)S(1)} %broadcast_in_dim.24), channel_id=1, replica_groups=mesh['node'=32,'feat'=4] {'node'}, dimensions={0} | all-to-all | bytes 256 | tf_op jit(solution)/shard_map/all_to_all | solution.py:30
  118.4 0.6 reduce_sum.59
  (48 shorter events, 4.3 us)
Async XLA Ops:
  0.6 0.8 copy-start
  2.5 23.9 %copy-start.4 = (s32[1,4]{1,0:T(1,128)S(1)}, s32[1,4]{1,0:T(1,128)}, u32[]{:S(2)}) copy-start(s32[1,4]{1,0:T(1,128)} %param.14) | copy-start | bytes 52
  24.5 17.1 %collective-permute-start = (bf16[64,1024]{1,0:T(8,128)(2,1)S(1)}, bf16[64,1024]{1,0:T(8,128)(2,1)S(1)}, u32[]{:S(2)}, u32[]{:S(2)}) collective-permute-start(bf16[64,1024]{1,0:T(8,128)(2,1)S(1)} %maximum_convert_fusion), channel_id=1, source_target_pairs={{0,124},{4,0},{8,4},{12,8},{16,12},{20,16},{24,20},{28,24},{32,28}... | collective-permute-start | bytes 393224 | tf_op jit(solution)/shard_map/ppermute | solution.py:13
  29.3 9.7 %copy-start.5 = (s32[1,4]{1,0:T(1,128)S(1)}, s32[1,4]{1,0:T(1,128)}, u32[]{:S(2)}) copy-start(s32[1,4]{1,0:T(1,128)} %param.15) | copy-start | bytes 52
  41.7 40.0 %copy-start.1 = (bf16[4096,1024]{1,0:T(8,128)(2,1)S(1)}, bf16[4096,1024]{1,0:T(8,128)(2,1)}, u32[]{:S(2)}) copy-start(bf16[4096,1024]{1,0:T(8,128)(2,1)} %convert.6) | copy-start | bytes 25165828
  41.7 8.9 %collective-permute-start.1 = (bf16[64,1024]{1,0:T(8,128)(2,1)S(1)}, bf16[64,1024]{1,0:T(8,128)(2,1)S(1)}, u32[]{:S(2)}, u32[]{:S(2)}) collective-permute-start(bf16[64,1024]{1,0:T(8,128)(2,1)S(1)} %get-tuple-element.6), channel_id=1, source_target_pairs={{0,120},{4,124},{8,0},{12,4},{16,8},{20,12},{24,16},{28,20},{32,24... | collective-permute-start | bytes 393224 | tf_op jit(solution)/shard_map/ppermute | solution.py:13
  49.8 4.2 %collective-permute-start.5 = (bf16[64,1024]{1,0:T(8,128)(2,1)S(1)}, bf16[64,1024]{1,0:T(8,128)(2,1)S(1)}, u32[]{:S(2)}, u32[]{:S(2)}) collective-permute-start(bf16[64,1024]{1,0:T(8,128)(2,1)S(1)} %get-tuple-element.8), channel_id=1, source_target_pairs={{0,120},{4,124},{8,0},{12,4},{16,8},{20,12},{24,16},{28,20},{32,24... | collective-permute-start | bytes 393224 | tf_op jit(solution)/shard_map/ppermute | solution.py:13
  50.1 13.7 %collective-permute-start.9 = (bf16[64,1024]{1,0:T(8,128)(2,1)S(1)}, bf16[64,1024]{1,0:T(8,128)(2,1)S(1)}, u32[]{:S(2)}, u32[]{:S(2)}) collective-permute-start(bf16[64,1024]{1,0:T(8,128)(2,1)S(1)} %get-tuple-element.7), channel_id=1, source_target_pairs={{0,120},{4,124},{8,0},{12,4},{16,8},{20,12},{24,16},{28,20},{32,24... | collective-permute-start | bytes 393224 | tf_op jit(solution)/shard_map/ppermute | solution.py:13
  50.6 13.4 %collective-permute-start.2 = (bf16[64,1024]{1,0:T(8,128)(2,1)S(1)}, bf16[64,1024]{1,0:T(8,128)(2,1)S(1)}, u32[]{:S(2)}, u32[]{:S(2)}) collective-permute-start(bf16[64,1024]{1,0:T(8,128)(2,1)S(1)} %broadcast_select_fusion.9), channel_id=1, source_target_pairs={{0,112},{4,116},{8,120},{12,124},{16,0},{20,4},{24,8},{28,12},{32,... | collective-permute-start | bytes 393224 | tf_op jit(solution)/shard_map/ppermute | solution.py:13
  54.0 10.0 %collective-permute-start.6 = (bf16[64,1024]{1,0:T(8,128)(2,1)S(1)}, bf16[64,1024]{1,0:T(8,128)(2,1)S(1)}, u32[]{:S(2)}, u32[]{:S(2)}) collective-permute-start(bf16[64,1024]{1,0:T(8,128)(2,1)S(1)} %broadcast_select_fusion.5), channel_id=1, source_target_pairs={{0,112},{4,116},{8,120},{12,124},{16,0},{20,4},{24,8},{28,12},{32,... | collective-permute-start | bytes 393224 | tf_op jit(solution)/shard_map/ppermute | solution.py:13
  63.9 6.4 %collective-permute-start.10 = (bf16[64,1024]{1,0:T(8,128)(2,1)S(1)}, bf16[64,1024]{1,0:T(8,128)(2,1)S(1)}, u32[]{:S(2)}, u32[]{:S(2)}) collective-permute-start(bf16[64,1024]{1,0:T(8,128)(2,1)S(1)} %broadcast_select_fusion.1), channel_id=1, source_target_pairs={{0,112},{4,116},{8,120},{12,124},{16,0},{20,4},{24,8},{28,12},{32,... | collective-permute-start | bytes 393224 | tf_op jit(solution)/shard_map/ppermute | solution.py:13
  64.0 6.3 %collective-permute-start.3 = (bf16[64,1024]{1,0:T(8,128)(2,1)S(1)}, bf16[64,1024]{1,0:T(8,128)(2,1)S(1)}, u32[]{:S(2)}, u32[]{:S(2)}) collective-permute-start(bf16[64,1024]{1,0:T(8,128)(2,1)S(1)} %broadcast_select_fusion.10), channel_id=1, source_target_pairs={{0,96},{4,100},{8,104},{12,108},{16,112},{20,116},{24,120},{28,124... | collective-permute-start | bytes 393224 | tf_op jit(solution)/shard_map/ppermute | solution.py:13
  64.1 8.3 %collective-permute-start.7 = (bf16[64,1024]{1,0:T(8,128)(2,1)S(1)}, bf16[64,1024]{1,0:T(8,128)(2,1)S(1)}, u32[]{:S(2)}, u32[]{:S(2)}) collective-permute-start(bf16[64,1024]{1,0:T(8,128)(2,1)S(1)} %broadcast_select_fusion.6), channel_id=1, source_target_pairs={{0,96},{4,100},{8,104},{12,108},{16,112},{20,116},{24,120},{28,124... | collective-permute-start | bytes 393224 | tf_op jit(solution)/shard_map/ppermute | solution.py:13
  70.2 6.0 %collective-permute-start.11 = (bf16[64,1024]{1,0:T(8,128)(2,1)S(1)}, bf16[64,1024]{1,0:T(8,128)(2,1)S(1)}, u32[]{:S(2)}, u32[]{:S(2)}) collective-permute-start(bf16[64,1024]{1,0:T(8,128)(2,1)S(1)} %broadcast_select_fusion.2), channel_id=1, source_target_pairs={{0,96},{4,100},{8,104},{12,108},{16,112},{20,116},{24,120},{28,124... | collective-permute-start | bytes 393224 | tf_op jit(solution)/shard_map/ppermute | solution.py:13
  70.3 11.8 %collective-permute-start.4 = (bf16[64,1024]{1,0:T(8,128)(2,1)S(1)}, bf16[64,1024]{1,0:T(8,128)(2,1)S(1)}, u32[]{:S(2)}, u32[]{:S(2)}) collective-permute-start(bf16[64,1024]{1,0:T(8,128)(2,1)S(1)} %broadcast_select_fusion.11), channel_id=1, source_target_pairs={{0,64},{4,68},{8,72},{12,76},{16,80},{20,84},{24,88},{28,92},{32,9... | collective-permute-start | bytes 393224 | tf_op jit(solution)/shard_map/ppermute | solution.py:13
  72.4 5.4 %collective-permute-start.8 = (bf16[64,1024]{1,0:T(8,128)(2,1)S(1)}, bf16[64,1024]{1,0:T(8,128)(2,1)S(1)}, u32[]{:S(2)}, u32[]{:S(2)}) collective-permute-start(bf16[64,1024]{1,0:T(8,128)(2,1)S(1)} %broadcast_select_fusion.7), channel_id=1, source_target_pairs={{0,64},{4,68},{8,72},{12,76},{16,80},{20,84},{24,88},{28,92},{32,9... | collective-permute-start | bytes 393224 | tf_op jit(solution)/shard_map/ppermute | solution.py:13
  76.3 5.4 %collective-permute-start.12 = (bf16[64,1024]{1,0:T(8,128)(2,1)S(1)}, bf16[64,1024]{1,0:T(8,128)(2,1)S(1)}, u32[]{:S(2)}, u32[]{:S(2)}) collective-permute-start(bf16[64,1024]{1,0:T(8,128)(2,1)S(1)} %broadcast_select_fusion.3), channel_id=1, source_target_pairs={{0,64},{4,68},{8,72},{12,76},{16,80},{20,84},{24,88},{28,92},{32,9... | collective-permute-start | bytes 393224 | tf_op jit(solution)/shard_map/ppermute | solution.py:13
  77.8 4.9 %copy-start.2 = (bf16[64,47]{0,1:T(8,128)(2,1)S(1)}, bf16[64,47]{0,1:T(8,128)(2,1)}, u32[]{:S(2)}) copy-start(bf16[64,47]{0,1:T(8,128)(2,1)} %param.18) | copy-start | bytes 18052
  77.8 5.1 %copy-start.3 = (bf16[64,47]{0,1:T(8,128)(2,1)S(1)}, bf16[64,47]{0,1:T(8,128)(2,1)}, u32[]{:S(2)}) copy-start(bf16[64,47]{0,1:T(8,128)(2,1)} %param.17) | copy-start | bytes 18052
  82.2 11.9 %copy-start.6 = (s32[1024]{0:T(1024)S(1)}, s32[1024]{0:T(1024)}, u32[]{:S(2)}) copy-start(s32[1024]{0:T(1024)} %param.19) | copy-start | bytes 12292
where the time goes:
time: 121 us
  blocking collectives  52.2 us (43%)
  waiting for transfers between devices  23.2 us (19%)
  starting transfers between devices  14.2 us (12%)
  other arithmetic  11.9 us (10%)
  matrix products  9.45 us (8%)
  between operations  6.99 us (6%)
  local copies, waits for them, and re-layouts  2.84 us (2%)
    all_to_all x2, blocking collectives, from_everyone(): lax.all_to_all(jnp.broadcast_to(value[None], (devices, *value.shape)), ax...  33.2 us
    ppermute x13, waiting for transfers between devices, from_behind(): return lax.ppermute(value, axis, pairs)  23.2 us
    all_to_all x1, blocking collectives, sum_at_owner(): lax.all_to_all(split_up(value, dim, devices), axis, 0, 0, tiled=True)  19 us
    ppermute x13, starting transfers between devices, from_behind(): return lax.ppermute(value, axis, pairs)  14.2 us
    another operation x1, other arithmetic  9.64 us
    dot_general x3, matrix products, contract(): lax.dot_general(weight, values, (((0,), (0,)), ((), ())), preferred_eleme...  4.06 us
    dot_general x3, matrix products, local(): term = jnp.dot(sources, rows, preferred_element_type=jnp.float32)  3.07 us
  transfers between devices with their start and end apart: 13, of which 8 were waited for; matrix products, arithmetic and copies ran while one was open for 13% of the time, Pallas kernels for 0%

commit v1 on v0

v1 whole, which is shorter than its diff:
```python
import functools

import jax
import jax.numpy as jnp
from jax import lax
from jax.experimental import pallas as pl
from jax.experimental.pallas import tpu as pltpu
from jax.sharding import PartitionSpec as P

FAN1 = 25
FAN2 = 10
MESH = pl.DeviceIdType.MESH
BF = jnp.bfloat16
F32 = jnp.float32
NODES = 32
FEAT = 4
ZN = 4
XN = 4


def kernel(
    feat_hbm, e1_hbm, w1s_hbm, w1n_hbm, need_hbm, live_hbm, e2_hbm, w2s_hbm, w2n_hbm, lab_hbm,
    loss_out, mean_out,
    feat_v, w1s_v, w1n_v, w2s_v, w2n_v, lab_v, need_s, live_s,
    e1_v, e2_v, e2_b, a_send, a_recv, w_buf, v_buf, wt, vt,
    sb, pc, zb, xb, lb, rb,
    in_sem, e1_sem, e2_sem, send_sem, a_sem, w_sem, v_sem, s_sem, pc_sem, z_sem, x_sem, l_sem, r_sem,
):
    n = lax.axis_index("node")
    f = lax.axis_index("feat")
    core = n % 2
    z = (n // 2) % ZN
    x = n // (2 * ZN)
    sends = []

    def send(src, dst, rsem, node, feat):
        copy = pltpu.make_async_remote_copy(
            src_ref=src, dst_ref=dst, send_sem=send_sem.at[len(sends)], recv_sem=rsem,
            device_id=(node, feat), device_id_type=MESH,
        )
        copy.start()
        sends.append(copy)

    def arrived(dst, rsem):
        pltpu.make_async_remote_copy(
            src_ref=dst, dst_ref=dst, send_sem=send_sem.at[0], recv_sem=rsem,
            device_id=(n, f), device_id_type=MESH,
        ).wait_recv()

    small = []
    for i, (src, dst) in enumerate([
        (feat_hbm, feat_v), (w1s_hbm, w1s_v), (w1n_hbm, w1n_v), (w2s_hbm, w2s_v), (w2n_hbm, w2n_v),
        (lab_hbm, lab_v), (need_hbm, need_s), (live_hbm, live_s),
    ]):
        c = pltpu.make_async_copy(src, dst, in_sem.at[i])
        c.start()
        small.append(c)
    e1c = []
    for i in range(4):
        c = pltpu.make_async_copy(e1_hbm.at[pl.ds(256 * i, 256), :], e1_v.at[pl.ds(256 * i, 256), :], e1_sem.at[i])
        c.start()
        e1c.append(c)
    e2c = []
    col = pl.multiple_of(f * 256, 256)
    for i in range(4):
        c = pltpu.make_async_copy(
            e2_hbm.at[pl.ds(1024 * i, 1024), pl.ds(col, 256)], e2_v.at[pl.ds(1024 * i, 1024), :], e2_sem.at[i])
        c.start()
        e2c.append(c)

    barrier = pltpu.get_barrier_semaphore()
    for d in range(1, NODES):
        pl.semaphore_signal(barrier, inc=1, device_id=((n + d) % NODES, f), device_id_type=MESH)
    for d in range(1, FEAT):
        pl.semaphore_signal(barrier, inc=1, device_id=(n, (f + d) % FEAT), device_id_type=MESH)

    for c in small:
        c.wait()
    w_buf[f, :, :] = jnp.zeros((64, 256), BF)
    w_buf[f, 0:25, :] = w1s_v[...]
    w_buf[f, 32:57, :] = w1n_v[...]
    v_buf[f, :, :] = jnp.zeros((64, 128), BF)
    v_buf[f, :, 0:47] = w2s_v[...]
    v_buf[f, :, 64:111] = w2n_v[...]
    a_send[...] = jnp.zeros((4, 64, 256), BF)
    acc = jnp.zeros((25, 1024), F32)
    feats = feat_v[...]
    for q in range(4):
        a_send[q, 0:25, :] = feats[:, 256 * q:256 * (q + 1)]
    for i in range(4):
        e1c[i].wait()
        rows = e1_v[256 * i:256 * (i + 1), :].astype(F32).astype(BF)
        acc = acc + jnp.dot(feats[:, 256 * i:256 * (i + 1)], rows, preferred_element_type=F32)
    agg = (acc / FAN1).astype(BF)
    for q in range(4):
        a_send[q, 32:57, :] = agg[:, 256 * q:256 * (q + 1)]

    pl.semaphore_wait(barrier, NODES - 1 + FEAT - 1)
    peers = [(f + d) % FEAT for d in (1, 3, 2)]
    for p in peers:
        send(w_buf.at[f], w_buf.at[f], w_sem.at[f], n, p)
    for p in peers:
        send(a_send.at[p], a_recv.at[f], a_sem.at[f], n, p)
    for p in peers:
        send(v_buf.at[f], v_buf.at[f], v_sem.at[f], n, p)
    a_recv[f, :, :] = a_send[f, :, :]

    for i in range(4):
        e2c[i].wait()
        e2_b[1024 * i:1024 * (i + 1), :] = e2_v[1024 * i:1024 * (i + 1), :].astype(F32).astype(BF)

    for p in peers:
        arrived(w_buf.at[p], w_sem.at[p])
    wt[...] = w_buf[...].reshape(256, 256).T
    for p in peers:
        arrived(a_recv.at[p], a_sem.at[p])
    before = jnp.dot(wt[...], a_recv[...].reshape(256, 256), preferred_element_type=F32)
    hidden = jnp.maximum(before, 0.0).astype(BF)
    for p in peers:
        arrived(v_buf.at[p], v_sem.at[p])
    vt[...] = v_buf[...].reshape(256, 128).T
    both = jnp.dot(vt[...], hidden, preferred_element_type=F32)
    logits = both[0:48, :]
    mine = both[64:112, :].astype(BF)
    sb[0, f, :, :] = mine
    pc[core, :, :] = mine

    partner = n + 1 - 2 * core
    send(pc.at[core], pc.at[core], pc_sem.at[0], partner, f)
    send(sb.at[0, f], sb.at[1, f], s_sem.at[1, f], (n + 16) % NODES, f)
    send(sb.at[0, f], sb.at[2, f], s_sem.at[2, f], (n + 1) % NODES, f)
    for p in peers:
        send(sb.at[0, f], sb.at[0, f], s_sem.at[0, f], n, p)

    source = (need_s[0, 3] + NODES) % NODES
    arrived(pc.at[1 - core], pc_sem.at[0])
    zb[z, :, :] = pc[source % 2]
    zpeers = [(z + d) % ZN for d in (1, 3, 2)]
    for q in zpeers:
        send(zb.at[z], zb.at[z], z_sem.at[z], x * 8 + q * 2 + core, f)
    for k in (1, 2):
        arrived(sb.at[k, f], s_sem.at[k, f])
        for p in peers:
            send(sb.at[k, f], sb.at[k, f], s_sem.at[k, f], n, p)
    for q in zpeers:
        arrived(zb.at[q], z_sem.at[q])
    xb[x, :, :] = zb[(source // 2) % ZN]
    xpeers = [(x + d) % XN for d in (1, 3, 2)]
    for q in xpeers:
        send(xb.at[x], xb.at[x], x_sem.at[x], q * 8 + z * 2 + core, f)
    gathered = jnp.zeros((48, 256), F32)

    def slot_term(k):
        term = jnp.zeros((48, 256), F32)
        for p in range(FEAT):
            r = 1024 * k + 256 * p
            term = term + jnp.dot(sb[k, p], e2_b[r:r + 256, :], preferred_element_type=F32)
        return term * live_s[0, k].astype(F32)

    for k in (0, 1, 2):
        for p in peers:
            arrived(sb.at[k, p], s_sem.at[k, p])
        gathered = gathered + slot_term(k)
    for q in xpeers:
        arrived(xb.at[q], x_sem.at[q])
    sb[3, f, :, :] = xb[source // (2 * ZN)]
    for p in peers:
        send(sb.at[3, f], sb.at[3, f], s_sem.at[3, f], n, p)
    for p in peers:
        arrived(sb.at[3, p], s_sem.at[3, p])
    gathered = gathered + slot_term(3)
    logits = logits + gathered / FAN2
    ids = lax.broadcasted_iota(jnp.int32, (48, 256), 0)
    lab = lab_v[f]
    lab = jnp.concatenate([lab[0:1, :], lab[1:2, :]], axis=1)
    picked = jnp.sum(jnp.where(ids == lab, logits, 0.0), axis=0, keepdims=True)
    total = jnp.sum(jnp.where(ids < 47, jnp.exp(logits), 0.0), axis=0, keepdims=True)
    loss = jnp.log(total) - picked
    lb[f, 0:1, :] = loss[:, 0:128]
    lb[f, 1:2, :] = loss[:, 128:256]
    for p in peers:
        send(lb.at[f], lb.at[f], l_sem.at[f], n, p)
    for p in peers:
        arrived(lb.at[p], l_sem.at[p])
    losses = lb[...]
    rb[n, :, :] = jnp.sum(jnp.sum(losses, axis=0), axis=0, keepdims=True)
    for d in range(1, NODES):
        q = (n + d) % NODES
        send(rb.at[n], rb.at[n], r_sem.at[n], q, f)
    out_copy = pltpu.make_async_copy(lb, loss_out, in_sem.at[0])
    out_copy.start()
    for d in range(1, NODES):
        q = (n + d) % NODES
        arrived(rb.at[q], r_sem.at[q])
    summed = jnp.sum(rb[...], axis=0)
    mean_out[...] = jnp.sum(summed, axis=1, keepdims=True) / (1024 * NODES)
    out_copy.wait()
    for copy in sends:
        copy.wait_send()


def local(features, edges_one, w1_self, w1_nbr, need_blocks, live_slots, edges_two, w2_self, w2_nbr, labels):
    any_spec = pl.BlockSpec(memory_space=pl.ANY)
    dma = pltpu.SemaphoreType.DMA
    loss, mean = pl.pallas_call(
        kernel,
        out_shape=(jax.ShapeDtypeStruct((4, 2, 128), F32), jax.ShapeDtypeStruct((1, 1), F32)),
        in_specs=[any_spec] * 10,
        out_specs=(any_spec, pl.BlockSpec(memory_space=pltpu.VMEM)),
        scratch_shapes=[
            pltpu.VMEM((25, 1024), BF), pltpu.VMEM((25, 256), BF), pltpu.VMEM((25, 256), BF),
            pltpu.VMEM((64, 47), BF), pltpu.VMEM((64, 47), BF), pltpu.VMEM((4, 2, 128), jnp.int32),
            pltpu.SMEM((1, 4), jnp.int32), pltpu.SMEM((1, 4), jnp.int32),
            pltpu.VMEM((1024, 1024), jnp.int32), pltpu.VMEM((4096, 256), jnp.int32), pltpu.VMEM((4096, 256), BF),
            pltpu.VMEM((4, 64, 256), BF), pltpu.VMEM((4, 64, 256), BF), pltpu.VMEM((4, 64, 256), BF),
            pltpu.VMEM((4, 64, 128), BF), pltpu.VMEM((256, 256), BF), pltpu.VMEM((128, 256), BF),
            pltpu.VMEM((4, 4, 48, 256), BF), pltpu.VMEM((2, 48, 256), BF), pltpu.VMEM((4, 48, 256), BF),
            pltpu.VMEM((4, 48, 256), BF), pltpu.VMEM((4, 2, 128), F32), pltpu.VMEM((NODES, 1, 128), F32),
            dma((8,)), dma((4,)), dma((4,)), dma((80,)), dma((4,)), dma((4,)), dma((4,)), dma((4, 4)),
            dma((1,)), dma((4,)), dma((4,)), dma((4,)), dma((NODES,)),
        ],
        compiler_params=pltpu.CompilerParams(collective_id=0, has_side_effects=True),
    )(features, edges_one, w1_self, w1_nbr, need_blocks, live_slots, edges_two, w2_self, w2_nbr,
      labels.reshape(4, 2, 128))
    return loss.reshape(1024), mean.reshape(())


def solution(mesh):
    return jax.shard_map(
        local,
        mesh=mesh,
        in_specs=(
            P("feat", "node"), P(None, "node"), P("feat", None), P("feat", None), P("node", None),
            P("node", None), P(None, "node"), P("feat", None), P("feat", None), P("node"),
        ),
        out_specs=(P("node"), P()),
        check_vma=False,
    )
```

time: 121 us -> 44.5 us (0.37)
  blocking collectives: 52.2 us -> 0 us
  Pallas kernels: 0 us -> 37.8 us
  waiting for transfers between devices: 23.2 us -> 0 us
  starting transfers between devices: 14.2 us -> 0 us
  other arithmetic: 11.9 us -> 0 us
  matrix products: 9.45 us -> 0 us
  between operations: 6.99 us -> 2.38 us
  local copies, waits for them, and re-layouts: 2.84 us -> 4.06 us
    all_to_all x3 -> x0, blocking collectives: 52.2 us -> none  [the longest x2 33.2 us: from_everyone(): lax.all_to_all(jnp.broadcast_to(value[None], (devices, *value.shape)), ax...]
    pallas_call x0 -> x1, Pallas kernels: none -> 37.8 us  [local(): pl.pallas_call(kernel, out_shape=(jax.ShapeDtypeStruct((4, 2, 128), F32),...]
    ppermute x13 -> x0, waiting for transfers between devices: 23.2 us -> none  [from_behind(): return lax.ppermute(value, axis, pairs)]
    ppermute x13 -> x0, starting transfers between devices: 14.2 us -> none  [from_behind(): return lax.ppermute(value, axis, pairs)]
    another operation x1 -> x0, other arithmetic: 9.64 us -> none
    dot_general x8 -> x0, matrix products: 9.45 us -> none  [the longest x3 4.06 us: contract(): lax.dot_general(weight, values, (((0,), (0,)), ((), ())), preferred_eleme...]
    unnamed x14 -> x3, local copies, waits for them, and re-layouts: 0.87 us -> 4.06 us
    reduce_sum x5 -> x0, other arithmetic: 2.01 us -> none  [the longest x1 1.2 us: local(): summed = taken_together(jnp.sum(node_loss), 'node')]
  transfers between devices with their start and end apart: 13 -> 0, of which waited for: 8 -> 0; matrix products, arithmetic and copies ran while one was open for 13% -> 0% of each run, Pallas kernels for 0% -> 0%
where the time goes in v1:
time: 44.5 us; the launch traced here: 44.2 us
  Pallas kernels  37.8 us (85%)
  local copies, waits for them, and re-layouts  4.06 us (9%)
  between operations  2.38 us (5%)
    pallas_call x1, Pallas kernels, local(): pl.pallas_call(kernel, out_shape=(jax.ShapeDtypeStruct((4, 2, 128), F32),...  37.8 us
    unnamed x3, local copies, waits for them, and re-layouts  4.06 us

profile of v1, /device:TPU:1, one launch (start us, length us, event | category | flops | bytes accessed | tf_op | source)
XLA Modules:
  0.0 44.2 jit_solution(12485691129937566130)
XLA Ops:
  0.6 1.4 %copy.12.w2s_hbm = bf16[64,47]{1,0:T(8,128)(2,1)} copy(bf16[64,47]{0,1:T(8,128)(2,1)} %param.17) | data formatting | bytes 12032 | tf_op args[7]
  2.0 1.4 %copy.13.w2n_hbm = bf16[64,47]{1,0:T(8,128)(2,1)} copy(bf16[64,47]{0,1:T(8,128)(2,1)} %param.18) | data formatting | bytes 12032 | tf_op args[8]
  3.4 37.8 %shard_map.113 = (f32[4,2,128]{2,1,0:T(2,128)}, f32[1,1]{1,0:T(1,128)}) custom-call(bf16[25,1024]{1,0:T(8,128)(2,1)} %feat_hbm.1, s32[1024,1024]{1,0:T(8,128)} %e1_hbm.1, bf16[25,256]{1,0:T(8,128)(2,1)} %w1s_hbm.1, bf16[25,256]{1,0:T(8,128)(2,1)} %w1n_hbm.1, s32[1,4]{1,0:T(1,128)} %need_hbm.1, s32[1,4]{1,0:T(1,128)} %live_hbm.1, s32[4096,1024]{1,0:T(8,128)} %e2_hbm.1, ...), custom_call_target="tpu_custom_call" | custom-call | tf_op jit(solution)/shard_map/pallas_call | solution.py:205
  41.2 1.3 %copy.16 = f32[1024]{0:T(1024)} copy(f32[1024]{0:T(1024)} %bitcast.4) | data formatting | bytes 8192

commit v2 on v1

v2 whole, which is shorter than its diff:
```python
import math

import jax
import jax.numpy as jnp
from jax import lax
from jax.experimental import pallas as pl
from jax.experimental.pallas import tpu as pltpu
from jax.sharding import PartitionSpec as P

FAN1 = 25
FAN2 = 10
MESH = pl.DeviceIdType.MESH
BF = jnp.bfloat16
F32 = jnp.float32
NODES = 32
FEAT = 4
ZN = 4
XN = 4


def kernel(
    feat_hbm, e1_hbm, w1s_hbm, w1n_hbm, need_hbm, live_hbm, e2_hbm, w2s_hbm, w2n_hbm, lab_hbm,
    loss_out, part_out,
    feat_v, w1s_v, w1n_v, w2s_v, w2n_v, lab_v, need_s, live_s,
    e1_v, e2_v, e2_b, a_send, a_recv, w_buf, v_buf, wt, vt,
    sb, lg, z1, x1, x2, z2, gath, lb, pb, rb,
    in_sem, e1_sem, e2_sem, send_sem, a_sem, w_sem, v_sem, n_sem, y_sem, lg_sem, p_sem, r_sem,
):
    n = lax.axis_index("node")
    f = lax.axis_index("feat")
    core = n % 2
    z = (n // 2) % ZN
    x = n // (2 * ZN)
    other = 1 - core
    partner = n + 1 - 2 * core
    sent = []

    def node(xx, zz, cc):
        return xx * (2 * ZN) + zz * 2 + cc

    def send(src, dst, rsem, to, feat, ssem=0):
        pltpu.make_async_remote_copy(
            src_ref=src, dst_ref=dst, send_sem=send_sem.at[ssem], recv_sem=rsem,
            device_id=(to, feat), device_id_type=MESH,
        ).start()
        if ssem == 0:
            sent.append(math.prod(src.shape) * src.dtype.itemsize)

    def arrived(dst, rsem):
        pltpu.make_async_remote_copy(
            src_ref=dst, dst_ref=dst, send_sem=send_sem.at[0], recv_sem=rsem,
            device_id=(n, f), device_id_type=MESH,
        ).wait_recv()

    peers = [(f + d) % FEAT for d in (2, 1, 3)]
    zpeers = [(z + d) % ZN for d in (2, 1, 3)]
    xpeers = [(x + d) % XN for d in (2, 1, 3)]
    three = pl.ds(0, 3)

    small = []
    for i, (src, dst) in enumerate([
        (w1s_hbm, w1s_v), (w1n_hbm, w1n_v), (w2s_hbm, w2s_v), (w2n_hbm, w2n_v), (feat_hbm, feat_v),
        (need_hbm, need_s), (live_hbm, live_s), (lab_hbm, lab_v),
    ]):
        c = pltpu.make_async_copy(src, dst, in_sem.at[i])
        c.start()
        small.append(c)
    barrier = pltpu.get_barrier_semaphore()

    def hello(to, feat):
        pl.semaphore_signal(barrier, inc=1, device_id=(to, feat), device_id_type=MESH)

    for p in peers:
        hello(n, p)
    for q in zpeers:
        hello(node(x, q, core), f)
        hello(node(x, q, other), f)
    for q in xpeers:
        hello(node(q, z, core), f)
        hello(node(q, z, other), f)
    hello(partner, f)
    hello((n + 1) % NODES, f)
    hello((n + NODES - 1) % NODES, f)
    e1c = []
    for i in range(4):
        c = pltpu.make_async_copy(e1_hbm.at[pl.ds(256 * i, 256), :], e1_v.at[pl.ds(256 * i, 256), :], e1_sem.at[i])
        c.start()
        e1c.append(c)
    for c in small:
        c.wait()
    for h in range(2):
        cols = slice(128 * h, 128 * (h + 1))
        w_buf[f, h, :, :] = jnp.zeros((64, 128), BF)
        w_buf[f, h, 0:25, :] = w1s_v[:, cols]
        w_buf[f, h, 32:57, :] = w1n_v[:, cols]
    v_buf[f, 0, :, 0:64] = w2s_v[0:24, :]
    v_buf[f, 0, :, 64:128] = w2n_v[0:24, :]
    v_buf[f, 1, 23:24, :] = jnp.zeros((1, 128), BF)
    v_buf[f, 1, 0:23, 0:64] = w2s_v[24:47, :]
    v_buf[f, 1, 0:23, 64:128] = w2n_v[24:47, :]
    a_send[...] = jnp.zeros((4, 64, 256), BF)
    feats = feat_v[...]
    for q in range(4):
        a_send[q, 0:25, :] = feats[:, 256 * q:256 * (q + 1)]
    pl.semaphore_wait(barrier, 18)
    for p in peers:
        send(w_buf.at[f, core], w_buf.at[f, core], w_sem.at[core], n, p)
    for p in peers:
        send(v_buf.at[f, core], v_buf.at[f, core], v_sem.at[core], n, p)
    for p in peers:
        send(a_send.at[p, pl.ds(0, 32)], a_recv.at[f, pl.ds(0, 32)], a_sem.at[0], n, p)
    acc = jnp.zeros((25, 1024), F32)
    for i in range(4):
        e1c[i].wait()
        rows = e1_v[256 * i:256 * (i + 1), :].astype(F32).astype(BF)
        acc = acc + jnp.dot(feats[:, 256 * i:256 * (i + 1)], rows, preferred_element_type=F32)
    agg = (acc / FAN1).astype(BF)
    for q in range(4):
        a_send[q, 32:57, :] = agg[:, 256 * q:256 * (q + 1)]
    for p in peers:
        send(a_send.at[p, pl.ds(32, 32)], a_recv.at[f, pl.ds(32, 32)], a_sem.at[1], n, p)
    a_recv[f, :, :] = a_send[f, :, :]
    e2c = []
    for i in range(4):
        c = pltpu.make_async_copy(
            e2_hbm.at[pl.ds(1024 * i, 1024), :], e2_v.at[pl.ds(1024 * i, 1024), :], e2_sem.at[i])
        c.start()
        e2c.append(c)
    arrived(w_buf.at[three, 0], w_sem.at[core])
    for p in peers:
        send(w_buf.at[p, core], w_buf.at[p, core], w_sem.at[core], partner, f)
    arrived(v_buf.at[three, 0], v_sem.at[core])
    for p in peers:
        send(v_buf.at[p, core], v_buf.at[p, core], v_sem.at[core], partner, f)
    arrived(w_buf.at[three, 0], w_sem.at[other])
    for h in range(2):
        wt[128 * h:128 * (h + 1), :] = w_buf[:, h, :, :].reshape(256, 128).T
    arrived(v_buf.at[three, 0], v_sem.at[other])
    for p in range(FEAT):
        for h in range(2):
            vt[24 * h:24 * (h + 1), 64 * p:64 * (p + 1)] = v_buf[p, h, :, 0:64]
            vt[48 + 24 * h:72 + 24 * h, 64 * p:64 * (p + 1)] = v_buf[p, h, :, 64:128]
    arrived(a_recv.at[three, pl.ds(0, 32)], a_sem.at[0])
    arrived(a_recv.at[three, pl.ds(0, 32)], a_sem.at[1])
    before = jnp.dot(wt[...], a_recv[...].reshape(256, 256), preferred_element_type=F32)
    hidden = jnp.maximum(before, 0.0).astype(BF)
    both = jnp.dot(vt[...], hidden, preferred_element_type=F32)
    lg[f, :, :] = both[0:48, :]
    mine = both[48:96, :].astype(BF)
    for h in range(2):
        half = mine[:, 128 * h:128 * (h + 1)]
        sb[0, f, h, :, :] = half
    z1[z * 2 + core, :, :] = mine[:, 0:128]
    x1[x * 2 + core, :, :] = mine[:, 128:256]
    for q, r in zip(zpeers, xpeers):
        for c in (core, other):
            send(sb.at[0, f, 0], z1.at[z * 2 + core], p_sem.at[0], node(x, q, c), f)
            send(sb.at[0, f, 1], x1.at[x * 2 + core], p_sem.at[1], node(r, z, c), f)
    send(sb.at[0, f, 0], z1.at[z * 2 + core], p_sem.at[0], partner, f)
    send(sb.at[0, f, 1], x1.at[x * 2 + core], p_sem.at[1], partner, f)
    send(sb.at[0, f], sb.at[1, f], n_sem.at[0], (n + 16) % NODES, f)
    send(sb.at[0, f], sb.at[2, f], n_sem.at[1], (n + 1) % NODES, f)
    for p in peers:
        send(sb.at[0, f], sb.at[0, f], y_sem.at[0], n, p)
    for p in peers:
        send(lg.at[f], lg.at[f], lg_sem.at[0], n, p)

    source = (need_s[0, 3] + NODES) % NODES
    offset = (source - n + NODES) % NODES
    from_core = source % 2
    from_z = (source // 2) % ZN
    from_x = source // (2 * ZN)
    low = (z * 2 + from_core - offset + NODES) % (2 * ZN)
    via_x = ((x * (2 * ZN) + low + offset) // (2 * ZN)) % XN

    def convert(k):
        e2c[k].wait()

        def rows(i, carry):
            at = pl.ds(pl.multiple_of(1024 * k + 64 * i, 64), 64)
            e2_b[at, :] = e2_v[at, :].astype(F32).astype(BF)
            return carry

        lax.fori_loop(0, 16, rows, 0)

    for k in range(4):
        convert(k)
    seven = pl.ds(0, 7)
    arrived(z1.at[seven], p_sem.at[0])
    x2[x, :, :] = z1[from_z * 2 + from_core]
    for r in xpeers:
        send(x2.at[x], x2.at[x], p_sem.at[2], node(r, z, core), f)
    arrived(x1.at[seven], p_sem.at[1])
    z2[z, :, :] = x1[via_x * 2 + from_core]
    for r in zpeers:
        send(z2.at[z], z2.at[z], p_sem.at[3], node(x, r, core), f)
    for k in (1, 2):
        arrived(sb.at[k, f], n_sem.at[k - 1])
        for p in peers:
            send(sb.at[k, f], sb.at[k, f], y_sem.at[k], n, p)

    def slot_term(k):
        pieces = jnp.concatenate([sb[k, p, h] for p in range(FEAT) for h in range(2)], axis=1)
        term = jnp.dot(pieces, e2_b[1024 * k:1024 * (k + 1), :], preferred_element_type=F32)
        return term * (live_s[0, k].astype(F32) / FAN2)

    arrived(sb.at[0, three], y_sem.at[0])
    arrived(lg.at[three], lg_sem.at[0])
    own = jnp.concatenate([lg[p] for p in range(FEAT)], axis=1)
    gath[...] = own + slot_term(0)
    arrived(x2.at[three], p_sem.at[2])
    sb[3, f, 0, :, :] = x2[from_x]
    arrived(z2.at[three], p_sem.at[3])
    sb[3, f, 1, :, :] = z2[from_z]
    for p in peers:
        send(sb.at[3, f], sb.at[3, f], y_sem.at[3], n, p)
    for k in (1, 2):
        arrived(sb.at[k, three], y_sem.at[k])
        gath[...] = gath[...] + slot_term(k)
    arrived(sb.at[3, three], y_sem.at[3])
    logits = gath[...] + slot_term(3)
    ids = lax.broadcasted_iota(jnp.int32, (48, 1024), 0)
    lab = jnp.concatenate([lab_v[i // 2, i % 2:i % 2 + 1, :] for i in range(8)], axis=1)
    picked = jnp.sum(jnp.where(ids == lab, logits, 0.0), axis=0, keepdims=True)
    total = jnp.sum(jnp.where(ids < 47, jnp.exp(logits), 0.0), axis=0, keepdims=True)
    loss = jnp.log(total) - picked
    part = loss[:, 0:128]
    for i in range(1, 8):
        part = part + loss[:, 128 * i:128 * (i + 1)]
    rb[n, :, :] = part
    for d in [16] + [d for d in range(1, NODES) if d != 16]:
        send(rb.at[n], rb.at[n], r_sem.at[0], (n + d) % NODES, f, 1)
    for i in range(8):
        lb[i // 2, i % 2:i % 2 + 1, :] = loss[:, 128 * i:128 * (i + 1)]
    loss_copy = pltpu.make_async_copy(lb, loss_out, in_sem.at[0])
    loss_copy.start()
    tiles = sum(sent) // 4096
    assert tiles * 4096 == sum(sent)
    done = e2_v.at[pl.ds(0, 8 * tiles), pl.ds(0, 128)]
    pltpu.make_async_copy(done, done, send_sem.at[0]).wait()
    loss_copy.wait()
    most = rb.at[pl.ds(0, NODES - 1)]
    arrived(most, r_sem.at[0])
    pb[...] = jnp.sum(rb[...], axis=0)
    part_copy = pltpu.make_async_copy(pb, part_out, in_sem.at[1])
    part_copy.start()
    pltpu.make_async_copy(most, most, send_sem.at[1]).wait()
    part_copy.wait()


def finish(loss_ref, part_ref, loss_out, mean_out):
    loss_out[...] = loss_ref[...]
    mean_out[...] = jnp.sum(part_ref[...], axis=1, keepdims=True) / (1024 * NODES)


def local(features, edges_one, w1_self, w1_nbr, need_blocks, live_slots, edges_two, w2_self, w2_nbr, labels):
    any_spec = pl.BlockSpec(memory_space=pl.ANY)
    vmem_spec = pl.BlockSpec(memory_space=pltpu.VMEM)
    dma = pltpu.SemaphoreType.DMA
    vmem = pltpu.VMEM
    loss, part = pl.pallas_call(
        kernel,
        out_shape=(jax.ShapeDtypeStruct((4, 2, 128), F32), jax.ShapeDtypeStruct((1, 128), F32)),
        in_specs=[any_spec] * 10,
        out_specs=(any_spec, any_spec),
        scratch_shapes=[
            vmem((25, 1024), BF), vmem((25, 256), BF), vmem((25, 256), BF),
            vmem((47, 64), BF), vmem((47, 64), BF), vmem((4, 2, 128), jnp.int32),
            pltpu.SMEM((1, 4), jnp.int32), pltpu.SMEM((1, 4), jnp.int32),
            vmem((1024, 1024), jnp.int32), vmem((4096, 1024), jnp.int32), vmem((4096, 1024), BF),
            vmem((4, 64, 256), BF), vmem((4, 64, 256), BF), vmem((4, 2, 64, 128), BF),
            vmem((4, 2, 24, 128), BF), vmem((256, 256), BF), vmem((96, 256), BF),
            vmem((4, 4, 2, 48, 128), BF), vmem((4, 48, 256), F32), vmem((8, 48, 128), BF), vmem((8, 48, 128), BF),
            vmem((4, 48, 128), BF), vmem((4, 48, 128), BF), vmem((48, 1024), F32),
            vmem((4, 2, 128), F32), vmem((1, 128), F32), vmem((NODES, 1, 128), F32),
            dma((8,)), dma((4,)), dma((4,)), dma((2,)), dma((2,)), dma((2,)), dma((2,)), dma((2,)), dma((4,)),
            dma((1,)), dma((4,)), dma((1,)),
        ],
        compiler_params=pltpu.CompilerParams(collective_id=0, has_side_effects=True),
    )(features, edges_one, w1_self, w1_nbr, need_blocks, live_slots, edges_two, w2_self.T, w2_nbr.T,
      labels.reshape(4, 2, 128))
    loss, mean = pl.pallas_call(
        finish,
        out_shape=(jax.ShapeDtypeStruct((4, 2, 128), F32), jax.ShapeDtypeStruct((1, 1), F32)),
        in_specs=[vmem_spec, vmem_spec],
        out_specs=(vmem_spec, vmem_spec),
    )(loss, part)
    return loss.reshape(1024), mean.reshape(())


def solution(mesh):
    return jax.shard_map(
        local,
        mesh=mesh,
        in_specs=(
            P("feat", "node"), P(None, "node"), P("feat", None), P("feat", None), P("node", None),
            P("node", None), P(None, "node"), P("feat", None), P("feat", None), P("node"),
        ),
        out_specs=(P("node"), P()),
        check_vma=False,
    )
```

time: 44.5 us -> 32.2 us (0.72)
  Pallas kernels: 37.8 us -> 31.3 us
  local copies, waits for them, and re-layouts: 4.06 us -> 0 us
  between operations: 2.38 us -> 0.64 us
    pallas_call x1, Pallas kernels: 37.8 us -> 30 us  [local(): pl.pallas_call(kernel, out_shape=(jax.ShapeDtypeStruct((4, 2, 128), F32),...]
    unnamed x3 -> x0, local copies, waits for them, and re-layouts: 4.06 us -> none
    pallas_call x0 -> x1, Pallas kernels: none -> 1.27 us  [local(): pl.pallas_call(finish, out_shape=(jax.ShapeDtypeStruct((4, 2, 128), F32),...]
where the time goes in v2:
time: 32.2 us; the launch traced here: 32 us
  Pallas kernels  31.3 us (97%)
  between operations  0.64 us (2%)
    pallas_call x1, Pallas kernels, local(): pl.pallas_call(kernel, out_shape=(jax.ShapeDtypeStruct((4, 2, 128), F32),...  30 us
    pallas_call x1, Pallas kernels, local(): pl.pallas_call(finish, out_shape=(jax.ShapeDtypeStruct((4, 2, 128), F32),...  1.27 us

profile of v2, /device:TPU:1, one launch (start us, length us, event | category | flops | bytes accessed | tf_op | source)
XLA Modules:
  0.0 32.0 jit_solution(2621084339557462284)
XLA Ops:
  0.6 30.0 %shard_map.113 = (f32[4,2,128]{2,1,0:T(2,128)}, f32[1,128]{1,0:T(1,128)}) custom-call(bf16[25,1024]{1,0:T(8,128)(2,1)} %feat_hbm.1, s32[1024,1024]{1,0:T(8,128)} %e1_hbm.1, bf16[25,256]{1,0:T(8,128)(2,1)} %w1s_hbm.1, bf16[25,256]{1,0:T(8,128)(2,1)} %w1n_hbm.1, s32[1,4]{1,0:T(1,128)} %need_hbm.1, s32[1,4]{1,0:T(1,128)} %live_hbm.1, s32[4096,1024]{1,0:T(8,128)} %e2_hbm.1, ...), custom_call_target="tpu_custom_call" | custom-call | tf_op jit(solution)/shard_map/pallas_call | solution.py:261
  30.7 1.3 %shard_map.114 = (f32[4,2,128]{2,1,0:T(2,128)}, f32[1,1]{1,0:T(1,128)}) custom-call(f32[4,2,128]{2,1,0:T(2,128)} %get-tuple-element.6.loss_ref, f32[1,128]{1,0:T(1,128)} %get-tuple-element.7.part_ref), custom_call_target="tpu_custom_call" | custom-call | tf_op jit(solution)/shard_map/pallas_call | solution.py:282
